TPU v7x, 32 devices: a whole 2x2x4 slice. The times are simulated.
32 devices in a mesh: seq: 4 (over x, core), tensor: 8 (over z, y).
Axes of the slice: x: 2, y: 2, z: 4, core: 2. Of those that a mesh axis runs over, the one named last changes fastest.
Arguments:
- token_ids: int32 [2, 7], replicated, may hold values from 0 to 131071
- cache_lengths: int32 [7], replicated, may hold values from 1 to 5118
- embed_table: bfloat16 [131072, 1024], P('seq', 'tensor'), may hold values from -64 to 64
- attn_gain: float32 [1024], replicated, may hold values from 0.1 to 1.9
- final_gain: float32 [1024], replicated, may hold values from 0.1 to 1.9
- w_qkv: bfloat16 [1024, 3, 1024], P(None, None, 'tensor'), may hold values from -0.1875 to 0.1875
- w_out: bfloat16 [1024, 1024], P('tensor'), may hold values from -0.1875 to 0.1875
- cache_keys: bfloat16 [7, 5120, 1024], P(None, 'seq', 'tensor'), may hold values from -300 to 300
- cache_values: bfloat16 [7, 5120, 1024], P(None, 'seq', 'tensor'), may hold values from -24 to 24
Outputs:
- hidden: bfloat16 [2, 7, 1024], P(None, None, 'tensor')
- new_kv: bfloat16 [2, 2, 7, 1024], P(None, None, None, 'tensor')
- logprobs: float32 [2, 7, 131072], P(None, None, ('seq', 'tensor'))
All inputs are finite; a program needn't handle non-finite values.
Results may differ from a plain program's by a relative error of at most 0.0085.
The roundings to bfloat16 on the way count: a program that leaves them out, or rounds other values in their place, can miss the bound.
Values may be sent and summed in bfloat16 or wider, within the bound.
A program may use at most 64 MiB of HBM per device.

v0:
```python
import math
import jax
import jax.numpy as jnp
from jax import lax
from jax.sharding import PartitionSpec as P

HD = 128
epsilon = 1e-05
logit_gain = 2.0


def combined_all(value, axis, join):
    pieces = jax.tree.map(lambda part: lax.all_gather(part, axis), value)
    head = jax.tree.map(lambda part: part[0], pieces)
    tail = jax.tree.map(lambda part: part[1:], pieces)
    running, _ = lax.scan(lambda running, share: (join(running, share), None), head, tail)
    return running


def rotate(vector, positions):
    half_size = vector.shape[-1] // 2
    frequency = 10000.0 ** (-(jnp.arange(half_size, dtype=jnp.float32) * 2.0 / vector.shape[-1]))
    angles = positions.astype(jnp.float32)[..., None] * frequency
    cosine_term = jnp.cos(angles)[:, :, None, :]
    sine_term = jnp.sin(angles)[:, :, None, :]
    first_half = vector[..., :half_size]
    second_half = vector[..., half_size:]
    return jnp.concatenate(
        [
            first_half * cosine_term - second_half * sine_term,
            first_half * sine_term + second_half * cosine_term,
        ],
        -1,
    )


def pair_join(earlier, later):
    highest = jnp.maximum(earlier[0], later[0])
    return (
        highest,
        earlier[1] * jnp.exp(earlier[0] - highest) + later[1] * jnp.exp(later[0] - highest),
    )


def body(
    token_ids,
    cache_lengths,
    embed_table,
    attn_gain,
    final_gain,
    w_qkv,
    w_out,
    cache_keys,
    cache_values,
):
    streams = token_ids.shape[1]
    vocab_rows, local_width = embed_table.shape
    model_width = attn_gain.shape[0]
    heads_here = local_width // HD
    slot_count = cache_keys.shape[1]
    seq_index = lax.axis_index("seq")
    tensor_index = lax.axis_index("tensor")
    local_ids = token_ids - seq_index * vocab_rows
    inside = (local_ids >= 0) & (local_ids < vocab_rows)
    picked = embed_table[jnp.clip(local_ids, 0, vocab_rows - 1)]
    picked = jnp.where(inside[..., None], picked, jnp.zeros_like(picked))
    embed_local = lax.psum(picked.astype(jnp.float32).astype(jnp.bfloat16), "seq").astype(
        jnp.float32
    )
    embed_whole = lax.all_gather(
        embed_local.astype(jnp.bfloat16), "tensor", axis=2, tiled=True
    ).astype(jnp.float32)
    normed = (
        embed_whole
        * lax.rsqrt(jnp.mean(embed_whole * embed_whole, -1, keepdims=True) + epsilon)
        * attn_gain
    ).astype(jnp.bfloat16)
    projected = jnp.einsum("sbd,dcf->sbcf", normed, w_qkv, preferred_element_type=jnp.float32)
    head_shape = (2, streams, heads_here, HD)
    positions = cache_lengths[None, :] + jnp.arange(2, dtype=jnp.int32)[:, None]
    queries = rotate(projected[:, :, 0].reshape(head_shape), positions).astype(jnp.bfloat16)
    new_keys = rotate(projected[:, :, 1].reshape(head_shape), positions).astype(jnp.bfloat16)
    new_values = projected[:, :, 2].reshape(head_shape).astype(jnp.bfloat16)
    new_kv = jnp.stack(
        [new_keys.reshape(2, streams, local_width), new_values.reshape(2, streams, local_width)]
    )
    inverse = HD ** (-0.5)
    key_rows = cache_keys.reshape(streams, slot_count, heads_here, HD)
    value_rows = cache_values.reshape(streams, slot_count, heads_here, HD)
    scores = (
        jnp.einsum("sbhe,bjhe->sbhj", queries, key_rows, preferred_element_type=jnp.float32)
        * inverse
    )
    slot_positions = seq_index * slot_count + jnp.arange(slot_count, dtype=jnp.int32)
    visible = (slot_positions[None, :] < cache_lengths[:, None])[None, :, None, :]
    local_max = jnp.max(jnp.where(visible, scores, -1e30), -1)
    weights = jnp.where(visible, jnp.exp(scores - local_max[..., None]), 0.0)
    local_sum = jnp.sum(weights, -1)
    local_out = jnp.einsum(
        "sbhj,bjhe->sbhe",
        weights,
        value_rows,
        preferred_element_type=jnp.float32,
        precision=lax.Precision.HIGHEST,
    )
    highest = lax.pmax(local_max, "seq")
    factor = jnp.exp(local_max - highest)
    cache_total, cache_out = lax.psum((local_sum * factor, local_out * factor[..., None]), "seq")
    fresh_scores = (
        jnp.einsum("sbhe,tbhe->sbht", queries, new_keys, preferred_element_type=jnp.float32)
        * inverse
    )
    allowed = (jnp.arange(2)[None, :] <= jnp.arange(2)[:, None])[:, None, None, :]
    fresh_max = jnp.max(jnp.where(allowed, fresh_scores, -1e30), -1)
    overall = jnp.maximum(highest, fresh_max)
    fresh_weights = jnp.where(allowed, jnp.exp(fresh_scores - overall[..., None]), 0.0)
    cache_scale = jnp.exp(highest - overall)
    denominator = cache_total * cache_scale + jnp.sum(fresh_weights, -1)
    numerator = cache_out * cache_scale[..., None] + jnp.einsum(
        "sbht,tbhe->sbhe",
        fresh_weights,
        new_values,
        preferred_element_type=jnp.float32,
        precision=lax.Precision.HIGHEST,
    )
    attended = (
        (numerator / denominator[..., None]).astype(jnp.bfloat16).reshape(2 * streams, local_width)
    )
    mixed_rows = jnp.dot(attended, w_out, preferred_element_type=jnp.float32).reshape(
        2, streams, model_width
    )
    mixed_local = lax.psum_scatter(mixed_rows, "tensor", scatter_dimension=2, tiled=True)
    hidden = (embed_local + mixed_local).astype(jnp.bfloat16)
    hidden_float = hidden.astype(jnp.float32)
    final_squares = lax.psum(jnp.sum(hidden_float * hidden_float, -1), "tensor")
    factor_rows = (
        lax.rsqrt(final_squares / model_width + epsilon) * (logit_gain / math.sqrt(model_width))
    ).reshape(2 * streams, 1)
    final_local = lax.dynamic_slice_in_dim(final_gain, tensor_index * local_width, local_width)
    gated_rows = (hidden_float * final_local).astype(jnp.bfloat16).reshape(2 * streams, local_width)
    partial_logits = lax.dot_general(
        gated_rows, embed_table, (((1,), (1,)), ((), ())), preferred_element_type=jnp.float32
    )
    shares = (
        lax.psum_scatter(partial_logits, "tensor", scatter_dimension=1, tiled=True) * factor_rows
    )
    share_max = jnp.max(shares, -1)
    share_sum = jnp.sum(jnp.exp(shares - share_max[:, None]), -1)
    vocab_max, vocab_sum = combined_all((share_max, share_sum), ("seq", "tensor"), pair_join)
    logprobs = shares - (vocab_max + jnp.log(vocab_sum))[:, None]
    return (hidden, new_kv, logprobs.reshape(2, streams, -1))


def solution(mesh):
    in_specs = (
        P(),
        P(),
        P("seq", "tensor"),
        P(),
        P(),
        P(None, None, "tensor"),
        P("tensor", None),
        P(None, "seq", "tensor"),
        P(None, "seq", "tensor"),
    )
    out_specs = (
        P(None, None, "tensor"),
        P(None, None, None, "tensor"),
        P(None, None, ("seq", "tensor")),
    )
    return jax.shard_map(body, mesh=mesh, in_specs=in_specs, out_specs=out_specs, check_vma=False)
```

profile of v0, /device:TPU:0, one launch (start us, length us, event | category | flops | bytes accessed | tf_op | source)
XLA Modules:
  0.0 251.6 jit_solution(10912633208323982474)
XLA Ops:
  7.2 0.8 compare_select_fusion
  8.1 0.7 compare_and_fusion
  9.5 0.7 broadcast_compare_fusion
  10.3 5.0 %gather_fusion = bf16[14,128]{1,0:T(8,128)(2,1)S(1)} fusion(bf16[32768,128]{1,0:T(8,128)(2,1)} %param.13, s32[1024]{0:T(1024)S(1)} %pad_clamp_fusion), kind=kCustom, calls=%fused_computation | custom fusion | bytes 7224 | tf_op jit(solution)/shard_map/gather | solution.py:65
  15.4 8.3 %psum.28 = bf16[2,7,128]{2,1,0:T(8,128)(2,1)S(1)} all-reduce(bf16[2,7,128]{2,1,0:T(8,128)(2,1)S(1)} %broadcast_select_fusion), channel_id=1, replica_groups=mesh['seq'=4,'tensor'=8] {'seq'}, use_global_device_ids=true, to_apply=%region_0.1 | all-reduce | flops 1792 | bytes 7168 | tf_op jit(solution)/shard_map/psum | solution.py:67
  23.7 26.4 %all_gather.15 = bf16[2,7,1024]{2,1,0:T(8,128)(2,1)S(1)} all-gather(bf16[2,7,128]{2,1,0:T(8,128)(2,1)S(1)} %psum.28), channel_id=1, replica_groups=mesh['seq'=4,'tensor'=8] {'tensor'}, dimensions={2}, use_global_device_ids=true | all-gather | bytes 32256 | tf_op jit(solution)/shard_map/all_gather | solution.py:70
  50.2 1.4 fusion.11
  51.8 0.8 select_reduce_fusion
  53.1 5.8 %pmax.7 = f32[2,7,1]{1,0,2:T(2,128)S(1)} all-reduce(f32[2,7,1]{1,0,2:T(2,128)S(1)} %bitcast.154), channel_id=1, replica_groups=mesh['seq'=4,'tensor'=8] {'seq'}, use_global_device_ids=true, to_apply=%region_3.4 | all-reduce | flops 14 | bytes 112 | tf_op jit(solution)/shard_map/pmax | solution.py:106
  59.5 2.7 %fusion.6 = f32[2,7,1,128]{3,0,1,2:T(2,128)S(1)} fusion(bf16[7,1280,128]{2,1,0:T(8,128)(2,1)} %param.19, f32[2,7,1,1280]{3,0,1,2:T(2,128)S(1)} %get-tuple-element.74, pred[7,1280]{1,0:T(8,128)(4,1)S(1)} %broadcast_compare_fusion, f32[2,7]{0,1:T(8,128)S(1)} %get-tuple-element.73, f32[2,7]{0,1:T(8,128)S(1)} %copy.54), kind=kOutput, calls=%fused_computation.12 | convolution fusion | flops 27562752 | bytes 2381680 | tf_op jit(solution)/shard_map/sbhj,bjhe->sbhe/dot_general | solution.py:99
  62.2 5.8 %all-reduce.3 = (f32[2,7,1,128]{3,0,1,2:T(2,128)S(1)}, f32[2,7,1]{1,0,2:T(2,128)S(1)}) all-reduce(f32[2,7,1,128]{3,0,1,2:T(2,128)S(1)} %fusion.6, f32[2,7,1]{1,0,2:T(2,128)S(1)} %get-tuple-element.70), channel_id=1, replica_groups=mesh['seq'=4,'tensor'=8] {'seq'}, use_global_device_ids=true, to_apply=%region_4.5 | all-reduce | flops 1806 | bytes 14448 | tf_op jit(solution)/shard_map/psum | solution.py:108
  68.4 0.8 fusion.13
  69.3 0.8 dynamic_slice.10
  70.1 53.2 %reduce-scatter.3.cloned.1.call-done = f32[2,7,128]{2,1,0:T(8,128)} async-done(((f32[2,7,1024]{2,1,0:T(8,128)}), f32[2,7,128]{2,1,0:T(8,128)}) %reduce-scatter.3.cloned.1.call-update) | async-done | bytes 7184 | tf_op jit(solution)/shard_map/reduce_scatter | solution.py:132
  123.3 0.8 fusion.33
  124.1 7.0 %fusion.62 = f32[14,32768]{1,0:T(8,128)} fusion(bf16[14,128]{1,0:T(8,128)(2,1)S(1)} %reshape.218, bf16[32768,128]{1,0:T(8,128)(2,1)} %param.13), kind=kOutput, calls=%fused_computation.106 | convolution fusion | flops 117440512 | bytes 10227200 | tf_op jit(solution)/shard_map/dot_general | solution.py:141
  131.8 19.6 %psum.31 = f32[2,7]{1,0:T(2,128)S(1)} all-reduce(f32[2,7]{1,0:T(2,128)S(1)} %get-tuple-element.58), channel_id=1, replica_groups=mesh['seq'=4,'tensor'=8] {'tensor'}, use_global_device_ids=true, to_apply=%region_12.13 | all-reduce | flops 14 | bytes 112 | tf_op jit(solution)/shard_map/psum | solution.py:135
  152.1 46.9 %reduce-scatter.5.cloned.1.call-done = f32[14,4096]{1,0:T(8,128)} async-done(((f32[14,32768]{1,0:T(8,128)}), f32[14,4096]{1,0:T(8,128)}) %reduce-scatter.5.cloned.1.call-update) | async-done | bytes 229392 | tf_op jit(solution)/shard_map/reduce_scatter | solution.py:145
  199.0 1.2 multiply_reduce_fusion
  200.4 1.2 exponential_reduce_fusion
  201.9 39.3 %all-reduce.2 = (f32[448]{0:T(512)S(1)}, f32[448]{0:T(512)S(1)}) all-reduce(f32[448]{0:T(512)S(1)} %dynamic-update-slice, f32[448]{0:T(512)S(1)} %dynamic-update-slice.1), channel_id=2, replica_groups=mesh['seq'=4,'tensor'=8] {'seq','tensor'}, use_global_device_ids=true, to_apply=%add | all-reduce | flops 896 | bytes 7168
  241.6 1.2 while.12
  242.8 1.0 multiply_subtract_fusion
  243.9 0.9 copy.69
  (85 shorter events, 5.7 us)
Async XLA Ops:
  7.2 44.7 %copy-start = (bf16[7,1280,128]{2,1,0:T(8,128)(2,1)S(1)}, bf16[7,1280,128]{2,1,0:T(8,128)(2,1)}, u32[]{:S(2)}) copy-start(bf16[7,1280,128]{2,1,0:T(8,128)(2,1)} %param.18) | copy-start | bytes 6881284
  7.2 116.1 %reduce-scatter.3.cloned.1.call-start = ((), (), s32[]{:S(2)}) async-start(), calls=%async_computation.2 | async-start | bytes 73728 | tf_op jit(solution)/shard_map/reduce_scatter | solution.py:132
  51.8 16.6 %copy-start.1 = (bf16[128,1024]{1,0:T(8,128)(2,1)S(1)}, bf16[128,1024]{1,0:T(8,128)(2,1)}, u32[]{:S(2)}) copy-start(bf16[128,1024]{1,0:T(8,128)(2,1)} %param.17) | copy-start | bytes 786436
  69.3 129.8 %reduce-scatter.5.cloned.1.call-start = ((), (), s32[]{:S(2)}) async-start(), calls=%async_computation.3 | async-start | bytes 2359296 | tf_op jit(solution)/shard_map/reduce_scatter | solution.py:145
Sparse Core Ops, SparseCore 0:
  69.4 53.8 reduce-scatter.2
  131.3 67.7 reduce-scatter.4
where the time goes:
time: 252 us
  blocking collectives  105 us (42%)
  waiting for transfers between devices  100 us (40%)
  between operations  14.2 us (6%)
  matrix products  13 us (5%)
  local copies, waits for them, and re-layouts  9.57 us (4%)
  other arithmetic  8.84 us (4%)
    reduce_scatter x1, waiting for transfers between devices, body(): lax.psum_scatter(mixed_rows, 'tensor', scatter_dimension=2, tiled=True)  53.2 us
    reduce_scatter x1, waiting for transfers between devices, body(): lax.psum_scatter(partial_logits, 'tensor', scatter_dimension=1, tiled=True)  46.9 us
    unnamed x1, blocking collectives  39.3 us
    all_gather x1, blocking collectives, body(): lax.all_gather(embed_local.astype(jnp.bfloat16), 'tensor', axis=2, tiled=...  26.4 us
    psum x1, blocking collectives, body(): final_squares = lax.psum(jnp.sum(hidden_float * hidden_float, -1), 'tensor')  19.6 us
    psum x1, blocking collectives, body(): lax.psum(picked.astype(jnp.float32).astype(jnp.bfloat16), 'seq')  8.35 us
    dot_general x1, matrix products, body(): lax.dot_general(gated_rows, embed_table, (((1,), (1,)), ((), ())), prefer...  7.03 us
    pmax x1, blocking collectives, body(): highest = lax.pmax(local_max, 'seq')  5.85 us
  transfers between devices with their start and end apart: 2, of which 2 were waited for; matrix products, arithmetic and copies ran while one was open for 1% of the time, Pallas kernels for 0%

commit v1 on v0

--- a/solution.py
+++ b/solution.py
@@ -1,12 +1,32 @@
+import functools
 import math
 import jax
 import jax.numpy as jnp
 from jax import lax
 from jax.sharding import PartitionSpec as P
+from jax.lax import axis_index, axis_size, ppermute
 
 HD = 128
 epsilon = 1e-05
 logit_gain = 2.0
+
+
+def return_all_the_circles(base_x, dev_axis):
+    known = axis_size(dev_axis)
+    carry_out = axis_index(dev_axis)
+    work_now, local_next = (known, carry_out)
+    y2, o_now = (base_x, 1)
+    while o_now < work_now:
+        w1 = tuple(((j0, j0 ^ o_now) for j0 in range(work_now)))
+        base_arr = ppermute(y2, axis_name=dev_axis, perm=w1)
+        carry = jnp.concatenate([y2, base_arr], 2)
+        current_value = jnp.concatenate([base_arr, y2], axis=2)
+        y2 = jnp.where(local_next & o_now == 0, carry, current_value)
+        o_now = 2 * o_now
+    return y2
+
+
+_prepare_roads = functools.partial(return_all_the_circles, dev_axis="tensor")
 
 
 def combined_all(value, axis, join):
@@ -67,9 +87,7 @@
     embed_local = lax.psum(picked.astype(jnp.float32).astype(jnp.bfloat16), "seq").astype(
         jnp.float32
     )
-    embed_whole = lax.all_gather(
-        embed_local.astype(jnp.bfloat16), "tensor", axis=2, tiled=True
-    ).astype(jnp.float32)
+    embed_whole = _prepare_roads(embed_local.astype(jnp.bfloat16)).astype(jnp.float32)
     normed = (
         embed_whole
         * lax.rsqrt(jnp.mean(embed_whole * embed_whole, -1, keepdims=True) + epsilon)

time: 252 us -> 238 us (0.944)
  blocking collectives: 105 us -> 79 us
  waiting for transfers between devices: 100 us -> 107 us
  starting transfers between devices: 0.08 us -> 5.89 us
    all_gather x1 -> x0, blocking collectives: 26.4 us -> none  [body(): lax.all_gather(embed_local.astype(jnp.bfloat16), 'tensor', axis=2, tiled=...]
    ppermute x0 -> x3, starting transfers between devices: none -> 5.81 us  [return_all_the_circles(): base_arr = ppermute(y2, axis_name=dev_axis, perm=w1)]
    ppermute x0 -> x3, waiting for transfers between devices: none -> 4.8 us  [return_all_the_circles(): base_arr = ppermute(y2, axis_name=dev_axis, perm=w1)]
  transfers between devices with their start and end apart: 2 -> 5, of which waited for: 2 -> 5; matrix products, arithmetic and copies ran while one was open for 1% -> 1% of each run, Pallas kernels for 0% -> 0%
where the time goes in v1:
time: 238 us; the launch traced here: 237 us
  waiting for transfers between devices  107 us (45%)
  blocking collectives  79 us (33%)
  between operations  14.2 us (6%)
  matrix products  13 us (5%)
  local copies, waits for them, and re-layouts  9.57 us (4%)
  other arithmetic  8.85 us (4%)
  starting transfers between devices  5.89 us (2%)
    reduce_scatter x1, waiting for transfers between devices, body(): lax.psum_scatter(mixed_rows, 'tensor', scatter_dimension=2, tiled=True)  55.2 us
    reduce_scatter x1, waiting for transfers between devices, body(): lax.psum_scatter(partial_logits, 'tensor', scatter_dimension=1, tiled=True)  46.5 us
    unnamed x1, blocking collectives  39.5 us
    psum x1, blocking collectives, body(): final_squares = lax.psum(jnp.sum(hidden_float * hidden_float, -1), 'tensor')  19.6 us
    psum x1, blocking collectives, body(): lax.psum(picked.astype(jnp.float32).astype(jnp.bfloat16), 'seq')  8.35 us
    dot_general x1, matrix products, body(): lax.dot_general(gated_rows, embed_table, (((1,), (1,)), ((), ())), prefer...  7.03 us
    psum x1, blocking collectives, body(): lax.psum((local_sum * factor, local_out * factor[..., None]), 'seq')  5.85 us
    ppermute x3, starting transfers between devices, return_all_the_circles(): base_arr = ppermute(y2, axis_name=dev_axis, perm=w1)  5.81 us
  transfers between devices with their start and end apart: 5, of which 5 were waited for; matrix products, arithmetic and copies ran while one was open for 1% of the time, Pallas kernels for 0%

profile of v1, /device:TPU:0, one launch (start us, length us, event | category | flops | bytes accessed | tf_op | source)
XLA Modules:
  0.0 237.5 jit_solution(908603169623369550)
XLA Ops:
  7.2 0.8 compare_select_fusion
  8.8 5.0 %gather_fusion = bf16[14,128]{1,0:T(8,128)(2,1)S(1)} fusion(bf16[32768,128]{1,0:T(8,128)(2,1)} %param.13, s32[1024]{0:T(1024)S(1)} %pad_clamp_fusion), kind=kCustom, calls=%fused_computation | custom fusion | bytes 7224 | tf_op jit(solution)/shard_map/gather | solution.py:85
  14.0 8.3 %psum.28 = bf16[2,7,128]{2,1,0:T(8,128)(2,1)S(1)} all-reduce(bf16[2,7,128]{2,1,0:T(8,128)(2,1)S(1)} %broadcast_select_fusion), channel_id=1, replica_groups=mesh['seq'=4,'tensor'=8] {'seq'}, use_global_device_ids=true, to_apply=%region_0.1 | all-reduce | flops 1792 | bytes 7168 | tf_op jit(solution)/shard_map/psum | solution.py:87
  22.3 1.6 collective-permute-start
  26.0 1.6 collective-permute-start.1
  27.6 2.1 collective-permute-done.1
  29.6 2.7 %collective-permute-start.2 = (bf16[2,7,512]{2,1,0:T(8,128)(2,1)S(1)}, bf16[2,7,512]{2,1,0:T(8,128)(2,1)S(1)}, u32[]{:S(2)}, u32[]{:S(2)}) collective-permute-start(bf16[2,7,512]{2,1,0:T(8,128)(2,1)S(1)} %maximum_select_fusion.1), channel_id=1, source_target_pairs={{0,4},{1,5},{2,6},{3,7},{4,0},{5,1},{6,2},{7,3},{8,12},{9,13},{10,... | collective-permute-start | bytes 43016 | tf_op jit(solution)/shard_map/ppermute | solution.py:21
  32.3 2.0 collective-permute-done.2
  34.5 1.4 fusion.11
  36.1 0.8 select_reduce_fusion
  37.3 5.7 %pmax.7 = f32[2,7,1]{1,0,2:T(2,128)S(1)} all-reduce(f32[2,7,1]{1,0,2:T(2,128)S(1)} %bitcast.154), channel_id=1, replica_groups=mesh['seq'=4,'tensor'=8] {'seq'}, use_global_device_ids=true, to_apply=%region_3.4 | all-reduce | flops 14 | bytes 112 | tf_op jit(solution)/shard_map/pmax | solution.py:124
  43.6 2.7 %fusion.6 = f32[2,7,1,128]{3,0,1,2:T(2,128)S(1)} fusion(bf16[7,1280,128]{2,1,0:T(8,128)(2,1)} %param.19, f32[2,7,1,1280]{3,0,1,2:T(2,128)S(1)} %get-tuple-element.74, pred[7,1280]{1,0:T(8,128)(4,1)S(1)} %broadcast_compare_fusion, f32[2,7]{0,1:T(8,128)S(1)} %get-tuple-element.73, f32[2,7]{0,1:T(8,128)S(1)} %copy.54), kind=kOutput, calls=%fused_computation.12 | convolution fusion | flops 27562752 | bytes 2381680 | tf_op jit(solution)/shard_map/sbhj,bjhe->sbhe/dot_general | solution.py:117
  46.4 5.8 %all-reduce.3 = (f32[2,7,1,128]{3,0,1,2:T(2,128)S(1)}, f32[2,7,1]{1,0,2:T(2,128)S(1)}) all-reduce(f32[2,7,1,128]{3,0,1,2:T(2,128)S(1)} %fusion.6, f32[2,7,1]{1,0,2:T(2,128)S(1)} %get-tuple-element.70), channel_id=1, replica_groups=mesh['seq'=4,'tensor'=8] {'seq'}, use_global_device_ids=true, to_apply=%region_4.5 | all-reduce | flops 1806 | bytes 14448 | tf_op jit(solution)/shard_map/psum | solution.py:126
  52.6 0.8 fusion.13
  54.2 55.2 %reduce-scatter.3.cloned.1.call-done = f32[2,7,128]{2,1,0:T(8,128)} async-done(((f32[2,7,1024]{2,1,0:T(8,128)}), f32[2,7,128]{2,1,0:T(8,128)}) %reduce-scatter.3.cloned.1.call-update) | async-done | bytes 7184 | tf_op jit(solution)/shard_map/reduce_scatter | solution.py:150
  110.2 7.0 %fusion.63 = f32[14,32768]{1,0:T(8,128)} fusion(bf16[14,128]{1,0:T(8,128)(2,1)S(1)} %reshape.218, bf16[32768,128]{1,0:T(8,128)(2,1)} %param.13), kind=kOutput, calls=%fused_computation.110 | convolution fusion | flops 117440512 | bytes 10227200 | tf_op jit(solution)/shard_map/dot_general | solution.py:159
  118.0 19.6 %psum.31 = f32[2,7]{1,0:T(2,128)S(1)} all-reduce(f32[2,7]{1,0:T(2,128)S(1)} %get-tuple-element.58), channel_id=1, replica_groups=mesh['seq'=4,'tensor'=8] {'tensor'}, use_global_device_ids=true, to_apply=%region_12.13 | all-reduce | flops 14 | bytes 112 | tf_op jit(solution)/shard_map/psum | solution.py:153
  138.2 46.5 %reduce-scatter.5.cloned.1.call-done = f32[14,4096]{1,0:T(8,128)} async-done(((f32[14,32768]{1,0:T(8,128)}), f32[14,4096]{1,0:T(8,128)}) %reduce-scatter.5.cloned.1.call-update) | async-done | bytes 229392 | tf_op jit(solution)/shard_map/reduce_scatter | solution.py:163
  184.8 1.2 multiply_reduce_fusion
  186.2 1.2 exponential_reduce_fusion
  187.6 39.5 %all-reduce.2 = (f32[448]{0:T(512)S(1)}, f32[448]{0:T(512)S(1)}) all-reduce(f32[448]{0:T(512)S(1)} %dynamic-update-slice, f32[448]{0:T(512)S(1)} %dynamic-update-slice.1), channel_id=2, replica_groups=mesh['seq'=4,'tensor'=8] {'seq','tensor'}, use_global_device_ids=true, to_apply=%add | all-reduce | flops 896 | bytes 7168
  227.4 1.2 while.12
  228.7 1.0 multiply_subtract_fusion
  229.8 0.9 copy.69
  (92 shorter events, 9.4 us)
Async XLA Ops:
  7.2 28.9 %copy-start = (bf16[7,1280,128]{2,1,0:T(8,128)(2,1)S(1)}, bf16[7,1280,128]{2,1,0:T(8,128)(2,1)}, u32[]{:S(2)}) copy-start(bf16[7,1280,128]{2,1,0:T(8,128)(2,1)} %param.18) | copy-start | bytes 6881284
  7.2 102.2 %reduce-scatter.3.cloned.1.call-start = ((), (), s32[]{:S(2)}) async-start(), calls=%async_computation.2 | async-start | bytes 73728 | tf_op jit(solution)/shard_map/reduce_scatter | solution.py:150
  22.3 3.7 %collective-permute-start = (bf16[2,7,128]{2,1,0:T(8,128)(2,1)S(1)}, bf16[2,7,128]{2,1,0:T(8,128)(2,1)S(1)}, u32[]{:S(2)}, u32[]{:S(2)}) collective-permute-start(bf16[2,7,128]{2,1,0:T(8,128)(2,1)S(1)} %psum.28), channel_id=1, source_target_pairs={{0,1},{1,0},{2,3},{3,2},{4,5},{5,4},{6,7},{7,6},{8,9},{9,8},{10,11... | collective-permute-start | bytes 10760 | tf_op jit(solution)/shard_map/ppermute | solution.py:21
  26.0 3.7 %collective-permute-start.1 = (bf16[2,7,256]{2,1,0:T(8,128)(2,1)S(1)}, bf16[2,7,256]{2,1,0:T(8,128)(2,1)S(1)}, u32[]{:S(2)}, u32[]{:S(2)}) collective-permute-start(bf16[2,7,256]{2,1,0:T(8,128)(2,1)S(1)} %maximum_select_fusion.2), channel_id=1, source_target_pairs={{0,2},{1,3},{2,0},{3,1},{4,6},{5,7},{6,4},{7,5},{8,10},{9,11},{10,... | collective-permute-start | bytes 21512 | tf_op jit(solution)/shard_map/ppermute | solution.py:21
  29.6 4.7 %collective-permute-start.2 = (bf16[2,7,512]{2,1,0:T(8,128)(2,1)S(1)}, bf16[2,7,512]{2,1,0:T(8,128)(2,1)S(1)}, u32[]{:S(2)}, u32[]{:S(2)}) collective-permute-start(bf16[2,7,512]{2,1,0:T(8,128)(2,1)S(1)} %maximum_select_fusion.1), channel_id=1, source_target_pairs={{0,4},{1,5},{2,6},{3,7},{4,0},{5,1},{6,2},{7,3},{8,12},{9,13},{10,... | collective-permute-start | bytes 43016 | tf_op jit(solution)/shard_map/ppermute | solution.py:21
  36.1 16.5 %copy-start.1 = (bf16[128,1024]{1,0:T(8,128)(2,1)S(1)}, bf16[128,1024]{1,0:T(8,128)(2,1)}, u32[]{:S(2)}) copy-start(bf16[128,1024]{1,0:T(8,128)(2,1)} %param.17) | copy-start | bytes 786436
  53.4 131.4 %reduce-scatter.5.cloned.1.call-start = ((), (), s32[]{:S(2)}) async-start(), calls=%async_computation.3 | async-start | bytes 2359296 | tf_op jit(solution)/shard_map/reduce_scatter | solution.py:163
Sparse Core Ops, SparseCore 0:
  53.5 55.8 reduce-scatter.2
  117.4 67.3 reduce-scatter.4
